TPU v7x, 32 devices: a whole 2x2x4 slice. The times are simulated.
32 devices in a mesh: chain: 8 (over z, core), bond: 4 (over y, x).
Axes of the slice: x: 2, y: 2, z: 4, core: 2. Of those that a mesh axis runs over, the one named last changes fastest.
Arguments:
- site_tensors: float32 [32, 256, 2, 256], P('chain', 'bond'), may hold values from -20 to 20
- bond_gates: float32 [32, 4, 4], P('chain'), may hold values from -1.5 to 2.5
Outputs:
- state: float32 [32, 256, 2, 256], P('chain', 'bond')
- profile: float32 [32], P('chain')
All inputs are finite; a program needn't handle non-finite values.
Results may differ from a plain program's by a relative error of at most 0.0002.
Values sent between devices are 32-bit elements; how exact they have to be, the bound alone decides.
A program may use at most 64 MiB of HBM per device.

v0:
```python
import functools
import math

import jax
import jax.numpy as jnp
from jax import lax
from jax.experimental import pallas as pl
from jax.experimental.pallas import tpu as pltpu
from jax.sharding import PartitionSpec as P

NS_ITERS = 3
RING = 4
CHUNKS = 4
LANES = 128
EPSILON = 1e-06


def split(value):
    high = value.astype(jnp.bfloat16)
    low = (value - high.astype(jnp.float32)).astype(jnp.bfloat16)
    return (high, low)


def times(a, b):
    (ah, al), (bh, bl) = (a, b)
    return jnp.dot(
        jnp.concatenate([ah, ah, al], axis=1),
        jnp.concatenate([bh, bl, bh], axis=0),
        preferred_element_type=jnp.float32,
    )


def times_transposed(a, b):
    (ah, al), (bh, bl) = (a, b)
    return lax.dot_general(
        jnp.concatenate([ah, ah, al], axis=1),
        jnp.concatenate([bh, bl, bh], axis=1),
        (((1,), (1,)), ((), ())),
        preferred_element_type=jnp.float32,
    )


def update(right, lefts, gate, on_left):
    width = right.shape[0]
    right_split = split(right)
    groups = []
    projected = []
    for left in lefts:
        left = left()
        r = left.shape[0] // 2
        theta = times(split(left), right_split) * (1.0 / math.sqrt(width))
        theta = [[theta[u * r:(u + 1) * r, v * width:(v + 1) * width] for v in range(2)] for u in range(2)]
        rows = []
        for s in range(2):
            row = []
            for t in range(2):
                total = None
                for u in range(2):
                    for v in range(2):
                        factor = gate[2 * s + t:2 * s + t + 1, 2 * u + v:2 * u + v + 1]
                        term = factor * theta[u][v]
                        total = term if total is None else total + term
                row.append(total)
            rows.append(jnp.concatenate(row, axis=1))
        group = split(jnp.concatenate(rows, axis=0))
        groups.append(group)
        projected.append(times_transposed(group, right_split))
    matrix = tuple(jnp.concatenate(part, axis=0) for part in zip(*groups))
    projected = jnp.concatenate(projected, axis=0)
    squares = jnp.sum(projected * projected, keepdims=True)
    iterate = projected * (1.0 / jnp.sqrt(squares + EPSILON))
    turned = split(iterate.T)
    iterate = split(iterate)
    gram = times_transposed(turned, turned)
    eye = jnp.where(
        lax.broadcasted_iota(jnp.int32, gram.shape, 0) == lax.broadcasted_iota(jnp.int32, gram.shape, 1),
        jnp.float32(1.5),
        jnp.float32(0.0),
    )
    carried = times(turned, matrix)
    factor = None
    for repeat in range(NS_ITERS):
        step = eye - 0.5 * gram
        factor = step if factor is None else times(split(factor), split(step))
        if repeat < NS_ITERS - 1:
            gram_split = split(gram)
            once = 1.5 * gram - 0.5 * times(gram_split, gram_split)
            gram = 1.5 * once - 0.5 * times(split(once), gram_split)
    factor = split(factor)
    on_left(math.sqrt(2 * width) * times(iterate, factor))
    carried = times(factor, split(carried))
    mean = jnp.sum(carried * carried, keepdims=True) * (1.0 / carried.size)
    scale_norm = jnp.sqrt(mean + EPSILON)
    return (carried * (1.0 / scale_norm), jnp.log(scale_norm))


def order(place):
    return place + (place // 2) * (1 - 2 * (place % 2))


def kernel(
    chains, bonds, rows, width,
    x_ref, gates_ref, out_ref, profile_ref,
    slab_sem, ring_sem, fetch_sem, xin, inbuf, gates, xbuf, recv, obuf, wall,
    g_send, g_recv, f_send, f_recv, gate_send, gate_recv,
    m_send, m_recv, h_send, h_recv, o_send, o_recv, w_send, w_recv,
):
    chain, bond = (lax.axis_index("chain"), lax.axis_index("bond"))
    slabs = chains // 2
    slab, core = (chain // 2, chain % 2)
    replica, ring = (bond // RING, order(bond % RING))
    tall = rows * 4
    height = width // CHUNKS
    sibling = {"chain": 2 * slab + 1 - core, "bond": bond}

    def remote(src, dst, send, recv_sem, chain_to, bond_to):
        return pltpu.make_async_remote_copy(
            src_ref=src, dst_ref=dst, send_sem=send, recv_sem=recv_sem,
            device_id={"chain": chain_to, "bond": bond_to},
            device_id_type=pl.DeviceIdType.MESH,
        )

    def landed(ref, sem):
        pltpu.make_async_copy(ref, ref, sem).wait()

    fetch = pltpu.make_async_copy(x_ref, xin, fetch_sem)
    fetch.start()
    gate_here = pltpu.make_async_copy(gates_ref, gates.at[core], gate_recv.at[core])
    gate_here.start()
    barrier = pltpu.get_barrier_semaphore()

    def greet(semaphore, chain_to, bond_to):
        to = {"chain": chain_to, "bond": bond_to}
        pl.semaphore_signal(semaphore, inc=1, device_id=to, device_id_type=pl.DeviceIdType.MESH)

    for db in range(1, bonds):
        greet(barrier, 2 * slab + 1, lax.rem(bond + db, bonds))

    @pl.when(core == 0)
    def _():
        greet(barrier, 2 * slab + 1, bond)

    for dz in range(1, slabs):
        for db in range(RING):
            greet(barrier, 2 * lax.rem(slab + dz, slabs), replica * RING + lax.rem(bond + db, RING))

    @pl.when(core == 1)
    def _():
        pl.semaphore_wait(barrier, 2 * bonds - 1)
        greet(slab_sem, 2 * slab, bond)

    @pl.when(core == 0)
    def _():
        pl.semaphore_wait(slab_sem, 1)

    gate_copy = remote(gates_ref, gates.at[core], gate_send, gate_recv.at[core], sibling["chain"], bond)
    gate_copy.start()
    fetch.wait()

    short = tall // 2
    gathers = []
    for i in (1, 0):
        for h in range(2):
            for j in range(2):
                for r in range(bonds // RING):
                    bond_to = r * RING + order(2 * core + j)
                    src = xin.at[pl.ds((2 * j + i) * tall + h * short, short)]
                    dst = inbuf.at[i, pl.ds(bond * tall + h * short, short)]
                    sem = g_recv.at[i, bond]
                    copy = remote(src, dst, g_send.at[i, h, j, r], sem, 2 * slab + h, bond_to)
                    here = pltpu.make_async_copy(src, dst, sem)
                    mine = jnp.logical_and(core == h, bond_to == bond)
                    gathers.append((copy, mine))
                    pl.when(mine)(here.start)
                    pl.when(jnp.logical_not(mine))(copy.start)

    forwards = []
    part = bonds // 2
    first = bond // part

    def receive(i, origins):
        for origin in origins:
            piece = inbuf.at[i, pl.ds(origin * tall + core * short, short)]
            landed(piece, g_recv.at[i, origin])
            copy = remote(
                piece, piece, f_send.at[i, origin], f_recv.at[i, origin], sibling["chain"], bond
            )
            copy.start()
            forwards.append(copy)
        for origin in origins:
            landed(inbuf.at[i, pl.ds(origin * tall + (1 - core) * short, short)], f_recv.at[i, origin])

    def spin(i, s, row, count):
        return jnp.concatenate(
            [inbuf[i, pl.ds(4 * row + 2 * t + s, count, stride=4), :] for t in range(2)], axis=1
        )

    def meet_ring():
        @pl.when(core == 0)
        def _():
            pl.semaphore_wait(barrier, (slabs - 1) * 2 * RING)
            greet(ring_sem, 2 * slab + 1, bond)

        @pl.when(core == 1)
        def _():
            pl.semaphore_wait(ring_sem, 1)

    passed = []

    def send_left(value):
        for g in range(2):
            for s in range(2):
                here = pl.ds((first + g * (1 - 2 * first)) * half, half)
                xbuf[s, here] = value[(2 * g + s) * half:(2 * g + s + 1) * half]
        before = lax.rem(ring + RING - 1, RING)
        slab_to = lax.rem(slab + slabs - jnp.where(ring == 0, 1, 0), slabs)
        bond_to = replica * RING + order(before)
        for q in range(CHUNKS):
            part = pl.ds(q * height, height)
            copy = remote(
                xbuf.at[core, part], recv.at[core, part], m_send.at[q], m_recv.at[q],
                2 * slab_to + core, bond_to,
            )
            copy.start()
            passed.append(copy)

    block = ring // 2
    half = width // 2

    def left_rows(g):
        which = first + g * (1 - 2 * first)
        receive(0, [which * part + lax.rem(bond + d, part) for d in range(part)])
        return jnp.concatenate([spin(0, s, which * half, half) for s in range(2)], axis=0)

    meet_ring()
    receive(1, [lax.rem(bond + d, bonds) for d in range(bonds)])
    landed(gates.at[0], gate_recv.at[0])
    landed(gates.at[1], gate_recv.at[1])
    right = jnp.concatenate([spin(1, s, 0, width) for s in range(2)], axis=1)
    lefts = [functools.partial(left_rows, g) for g in range(2)]
    new_right, weight_even = update(right, lefts, gates[block, 2 * (ring % 2)], send_left)

    for q in range(CHUNKS):
        part = recv.at[core, pl.ds(q * height, height)]
        landed(part, m_recv.at[q])
        copy = remote(part, part, h_send.at[q], h_recv.at[q], sibling["chain"], bond)
        copy.start()
        forwards.append(copy)
    for q in range(CHUNKS):
        landed(recv.at[1 - core, pl.ds(q * height, height)], h_recv.at[q])

    outs = []

    def put(h, value_of):
        for s in range(2):
            for t in range(2):
                obuf[h, pl.ds(2 * t + s, width, stride=4), :] = value_of(s, t)
        site = lax.rem(slab * 2 * RING + 2 * ring + 1 + h, 4 * chains)
        chain_to, slot = (site // 4, site % 4)
        for j in range(2):
            bond_to = replica * RING + 2 * j + core
            src = obuf.at[h, pl.ds(bond_to * tall, tall)]
            dst = out_ref.at[pl.ds(slot * tall, tall)]
            copy = remote(src, dst, o_send.at[h, j], o_recv.at[slot], chain_to, bond_to)
            here = pltpu.make_async_copy(src, dst, o_recv.at[slot])
            mine = jnp.logical_and(chain_to == chain, bond_to == bond)
            outs.append((copy, mine))
            pl.when(mine)(here.start)
            pl.when(jnp.logical_not(mine))(copy.start)

    def put_left(value):
        put(0, lambda s, t: value[s * width:(s + 1) * width, t * LANES:(t + 1) * LANES])

    left = jnp.concatenate([new_right[:, :width], new_right[:, width:]], axis=0)
    right = jnp.concatenate([recv[0], recv[1]], axis=1)
    new_right, weight_odd = update(right, [lambda: left], gates[block, 2 * (ring % 2) + 1], put_left)

    row = lax.broadcasted_iota(jnp.int32, (8, LANES), 0)
    lane = lax.broadcasted_iota(jnp.int32, (8, LANES), 1)
    own = wall.at[slab * RING + ring]
    own[...] = jnp.where(row == 0, weight_even, weight_odd)
    weights = []
    for dz in range(slabs):
        for dk in range(RING):
            if dz == 0 and dk == 0:
                continue
            chain_to = 2 * lax.rem(slab + dz, slabs) + core
            bond_to = replica * RING + order(lax.rem(ring + dk, RING))
            at = dz * RING + dk
            copy = remote(own, own, w_send.at[at], w_recv.at[at], chain_to, bond_to)
            copy.start()
            weights.append((copy, dz, dk))
    put(1, lambda s, t: new_right[:, s * width + t * LANES:s * width + (t + 1) * LANES])
    for copy, dz, dk in weights:
        source = lax.rem(slab + slabs - dz, slabs) * RING + lax.rem(ring + RING - dk, RING)
        landed(wall.at[source], w_recv.at[dz * RING + dk])
    total = jnp.zeros((8, LANES), jnp.float32)
    for e in range(slabs * RING):
        counted = jnp.logical_and(row < 2, 2 * e + row <= 4 * chain + lane)
        total = total + jnp.where(counted, wall[e], 0.0)
    running = jnp.sum(total, axis=0, keepdims=True) * (1.0 / (4 * chains))
    profile_ref[...] = jnp.broadcast_to(running, (8, LANES))

    for slot in range(4):
        landed(out_ref.at[pl.ds(slot * tall, tall)], o_recv.at[slot])
    for copy, mine in gathers:
        pl.when(jnp.logical_not(mine))(copy.wait_send)
    gate_copy.wait_send()
    for copy in forwards + passed + [c for c, dz, dk in weights]:
        copy.wait_send()
    for copy, mine in outs:
        pl.when(jnp.logical_not(mine))(copy.wait_send)


def per_device(chains, bonds, site_tensors, bond_gates):
    sites, rows, spins, width = site_tensors.shape
    assert sites == 4 and spins == 2 and width == 2 * LANES and bonds % RING == 0 and chains % 2 == 0
    cut = (sites, rows, spins, width // LANES, LANES)
    flat = site_tensors.reshape(cut).transpose(0, 1, 3, 2, 4).reshape(sites * rows * 4, LANES)
    slabs = chains // 2
    dma = pltpu.SemaphoreType.DMA
    out, profile = pl.pallas_call(
        functools.partial(kernel, chains, bonds, rows, width),
        out_shape=(
            jax.ShapeDtypeStruct(flat.shape, jnp.float32),
            jax.ShapeDtypeStruct((8, LANES), jnp.float32),
        ),
        in_specs=[pl.BlockSpec(memory_space=pltpu.HBM)] * 2,
        out_specs=(pl.BlockSpec(memory_space=pl.ANY), pl.BlockSpec(memory_space=pltpu.VMEM)),
        scratch_shapes=[
            pltpu.SemaphoreType.REGULAR,
            pltpu.SemaphoreType.REGULAR,
            dma,
            pltpu.VMEM(flat.shape, jnp.float32),
            pltpu.VMEM((2, 4 * width, LANES), jnp.float32),
            pltpu.VMEM((2,) + bond_gates.shape, jnp.float32),
            pltpu.VMEM((2, width, width), jnp.float32),
            pltpu.VMEM((2, width, width), jnp.float32),
            pltpu.VMEM((2, 4 * width, LANES), jnp.float32),
            pltpu.VMEM((slabs * RING, 8, LANES), jnp.float32),
            dma((2, 2, 2, bonds // RING)), dma((2, bonds)),
            dma((2, bonds)), dma((2, bonds)),
            dma, dma((2,)),
            dma((CHUNKS,)), dma((CHUNKS,)),
            dma((CHUNKS,)), dma((CHUNKS,)),
            dma((2, 2)), dma((4,)),
            dma((slabs * RING,)), dma((slabs * RING,)),
        ],
        compiler_params=pltpu.CompilerParams(
            has_side_effects=True, collective_id=0, vmem_limit_bytes=56_000_000
        ),
    )(flat, bond_gates)
    cut = (sites, rows, width // LANES, spins, LANES)
    state = out.reshape(cut).transpose(0, 1, 3, 2, 4).reshape(site_tensors.shape)
    return (state, profile[0, :sites])


def solution(mesh):
    chains, bonds = (mesh.shape["chain"], mesh.shape["bond"])
    return jax.shard_map(
        functools.partial(per_device, chains, bonds),
        mesh=mesh,
        in_specs=(P("chain", "bond", None, None), P("chain", None, None)),
        out_specs=(P("chain", "bond", None, None), P("chain")),
        check_vma=False,
    )
```

profile of v0, /device:TPU:11, one launch (start us, length us, event | category | flops | bytes accessed | tf_op | source)
XLA Modules:
  0.0 45.0 jit_solution(12360601763123102159)
XLA Ops:
  0.6 0.0 copy-start
  0.6 0.7 %copy-done = f32[4,4,4]{2,1,0:T(4,128)S(1)} copy-done((f32[4,4,4]{2,1,0:T(4,128)S(1)}, f32[4,4,4]{2,1,0:T(4,128)}, u32[]{:S(2)}) %copy-start) | copy-done | bytes 280
  1.3 42.4 %shard_map.41 = (f32[1024,128]{1,0:T(8,128)S(1)}, f32[8,128]{1,0:T(8,128)S(1)}) custom-call(f32[1024,128]{1,0:T(8,128)} %bitcast.13, f32[4,4,4]{2,1,0:T(4,128)S(1)} %copy-done), custom_call_target="tpu_custom_call" | custom-call | tf_op jit(solution)/shard_map/pallas_call | solution.py:322
  43.7 0.5 %slice_bitcast_fusion = f32[4]{0:T(128)} fusion(f32[8,128]{1,0:T(8,128)S(1)} %get-tuple-element.5), kind=kLoop, calls=%fused_computation | loop fusion | bytes 32 | tf_op jit(solution)/shard_map/squeeze | solution.py:355
  44.2 0.8 %copy.7 = f32[4,64,2,256]{3,2,1,0:T(2,128)} copy(f32[4,64,2,256]{3,2,1,0:T(2,128)S(1)} %bitcast.12) | data formatting | bytes 1048576
Async XLA Ops:
  0.6 0.7 %copy-start = (f32[4,4,4]{2,1,0:T(4,128)S(1)}, f32[4,4,4]{2,1,0:T(4,128)}, u32[]{:S(2)}) copy-start(f32[4,4,4]{2,1,0:T(4,128)} %gates_ref.1) | copy-start | bytes 772
where the time goes:
time: 45.2 us; the launch traced here: 45 us
  Pallas kernels  42.4 us (94%)
  local copies, waits for them, and re-layouts  2 us (4%)
  between operations  0.65 us (1%)
    pallas_call x1, Pallas kernels, per_device(): pl.pallas_call(functools.partial(kernel, chains, bonds, rows, width), out...  42.4 us
    unnamed x3, local copies, waits for them, and re-layouts  1.48 us

commit v1 on v0

v1 whole, which is shorter than its diff:
```python
import functools
import math

import jax
import jax.numpy as jnp
from jax import lax
from jax.experimental import pallas as pl
from jax.experimental.pallas import tpu as pltpu
from jax.sharding import PartitionSpec as P

NS_ITERS = 3
RING = 4
GROUPS = 4
LANES = 128
EPSILON = 1e-06


def split(value):
    high = value.astype(jnp.bfloat16)
    low = (value - high.astype(jnp.float32)).astype(jnp.bfloat16)
    return (high, low)


def dot(a, b):
    return jnp.dot(a, b, preferred_element_type=jnp.float32)


def dot_t(a, b):
    return lax.dot_general(a, b, (((1,), (1,)), ((), ())), preferred_element_type=jnp.float32)


def times(a, b):
    (ah, al), (bh, bl) = (a, b)
    return dot(ah, bh) + dot(al, bh) + dot(ah, bl)


def times_transposed(a, b):
    (ah, al), (bh, bl) = (a, b)
    return dot_t(ah, bh) + dot_t(al, bh) + dot_t(ah, bl)


def mixed(theta, gate, width):
    r = theta.shape[0] // 2
    theta = [[theta[u * r:(u + 1) * r, v * width:(v + 1) * width] for v in range(2)] for u in range(2)]
    scaled = gate * (1.0 / math.sqrt(width))
    rows = []
    for s in range(2):
        row = []
        for t in range(2):
            total = None
            for u in range(2):
                for v in range(2):
                    factor = scaled[2 * s + t:2 * s + t + 1, 2 * u + v:2 * u + v + 1]
                    term = factor * theta[u][v]
                    total = term if total is None else total + term
            row.append(total)
        rows.append(jnp.concatenate(row, axis=1))
    return jnp.concatenate(rows, axis=0)


def newton_schulz(gram, fill=()):
    assert NS_ITERS == 3
    fill = list(fill)

    def filled(value):
        if fill:
            fill.pop(0)()
        return value

    eye = jnp.where(
        lax.broadcasted_iota(jnp.int32, gram.shape, 0) == lax.broadcasted_iota(jnp.int32, gram.shape, 1),
        jnp.float32(1.5),
        jnp.float32(0.0),
    )
    factor = None
    for repeat in range(NS_ITERS):
        step = eye - 0.5 * gram
        factor = step if factor is None else times(split(factor), split(step))
        if repeat < NS_ITERS - 1:
            gram_split = split(gram)
            once = 1.5 * gram - 0.5 * filled(times(gram_split, gram_split))
            gram = 1.5 * once - 0.5 * filled(times(split(once), gram_split))
    while fill:
        fill.pop(0)()
    return split(factor)


def sum_of_squares(value):
    return jnp.sum(value * value, keepdims=True)


def norm_of(carried):
    mean = sum_of_squares(carried) * (1.0 / carried.size)
    return jnp.sqrt(mean + EPSILON)


def order(place):
    return place + (place // 2) * (1 - 2 * (place % 2))


def grouped(mine, d):
    if d == 0:
        return mine
    if d == 1:
        return mine + 1 - 2 * (mine % 2)
    if d == 2:
        return lax.rem(mine + 2, 4)
    return 3 - mine


def kernel(
    chains, bonds, rows, width,
    x_ref, gates_ref, out_ref, profile_ref,
    slab_sem, ring_sem, fetch_sem, xin, inbuf, gates, rsend, rrecv, obuf, wall,
    bh, bl, th, tl, mh, ml, ph, pl_, lh, ll, nh, nl, uh, ul, kept,
    g_send, g_recv, f_send, f_recv, gate_send, gate_recv,
    m_send, m_recv, h_send, h_recv, o_send, o_recv, w_send, w_recv,
):
    chain, bond = (lax.axis_index("chain"), lax.axis_index("bond"))
    slabs = chains // 2
    slab, core = (chain // 2, chain % 2)
    tall = rows * 4
    sibling = {"chain": 2 * slab + 1 - core, "bond": bond}
    replica = bond // RING

    def place_of(ring_at, slab_at):
        return order(lax.rem(ring_at + 3 * slab_at, RING))

    ring = lax.rem(order(bond % RING) + slab, RING)

    def remote(src, dst, send, recv_sem, chain_to, bond_to):
        return pltpu.make_async_remote_copy(
            src_ref=src, dst_ref=dst, send_sem=send, recv_sem=recv_sem,
            device_id={"chain": chain_to, "bond": bond_to},
            device_id_type=pl.DeviceIdType.MESH,
        )

    def landed(ref, sem):
        pltpu.make_async_copy(ref, ref, sem).wait()

    fetch = pltpu.make_async_copy(x_ref, xin, fetch_sem)
    fetch.start()
    gate_here = pltpu.make_async_copy(gates_ref, gates.at[core], gate_recv.at[core])
    gate_here.start()
    barrier = pltpu.get_barrier_semaphore()

    def greet(semaphore, chain_to, bond_to):
        to = {"chain": chain_to, "bond": bond_to}
        pl.semaphore_signal(semaphore, inc=1, device_id=to, device_id_type=pl.DeviceIdType.MESH)

    for db in range(1, bonds):
        greet(barrier, 2 * slab + 1, lax.rem(bond + db, bonds))

    @pl.when(core == 0)
    def _():
        greet(barrier, 2 * slab + 1, bond)

    for dz in range(1, slabs):
        for db in range(RING):
            greet(barrier, 2 * lax.rem(slab + dz, slabs), replica * RING + lax.rem(bond + db, RING))

    @pl.when(core == 1)
    def _():
        pl.semaphore_wait(barrier, 2 * bonds - 1)
        greet(slab_sem, 2 * slab, bond)

    @pl.when(core == 0)
    def _():
        pl.semaphore_wait(slab_sem, 1)

    gate_copy = remote(gates_ref, gates.at[core], gate_send, gate_recv.at[core], sibling["chain"], bond)
    gate_copy.start()
    fetch.wait()

    short = tall // 2
    gathers = []
    for i in (1, 0):
        for h in range(2):
            for j in range(2):
                for r in range(bonds // RING):
                    bond_to = r * RING + place_of(2 * core + j, slab)
                    src = xin.at[pl.ds((2 * j + i) * tall + h * short, short)]
                    dst = inbuf.at[i, pl.ds(bond * tall + h * short, short)]
                    sem = g_recv.at[i, bond]
                    copy = remote(src, dst, g_send.at[i, h, j, r], sem, 2 * slab + h, bond_to)
                    here = pltpu.make_async_copy(src, dst, sem)
                    mine = jnp.logical_and(core == h, bond_to == bond)
                    gathers.append((copy, mine))
                    pl.when(mine)(here.start)
                    pl.when(jnp.logical_not(mine))(copy.start)

    forwards = []
    part = bonds // GROUPS
    tier = width // GROUPS

    def members(d):
        return [grouped(bond // part, d) * part + lax.rem(bond + e, part) for e in range(part)]

    def pass_on(i, d):
        for origin in members(d):
            piece = inbuf.at[i, pl.ds(origin * tall + core * short, short)]
            landed(piece, g_recv.at[i, origin])
            copy = remote(
                piece, piece, f_send.at[i, origin], f_recv.at[i, origin], sibling["chain"], bond
            )
            copy.start()
            forwards.append(copy)

    def complete(i, d):
        for origin in members(d):
            landed(inbuf.at[i, pl.ds(origin * tall + (1 - core) * short, short)], f_recv.at[i, origin])

    def spin(i, s, row, count):
        return jnp.concatenate(
            [inbuf[i, pl.ds(4 * row + 2 * t + s, count, stride=4), :] for t in range(2)], axis=1
        )

    block = ring // 2
    before = lax.rem(ring + RING - 1, RING)
    slab_to = lax.rem(slab + slabs - jnp.where(ring == 0, 1, 0), slabs)
    prev_bond = replica * RING + place_of(before, slab_to)
    after = lax.rem(ring + 1, RING)
    slab_from = lax.rem(slab + jnp.where(ring == RING - 1, 1, 0), slabs)
    next_bond = replica * RING + place_of(after, slab_from)

    pass_on(1, 0)
    pass_on(0, 0)
    for d in range(1, GROUPS):
        pass_on(1, d)
    for d in range(GROUPS):
        complete(1, d)
    landed(gates.at[0], gate_recv.at[0])
    landed(gates.at[1], gate_recv.at[1])
    right = jnp.concatenate([spin(1, s, 0, width) for s in range(2)], axis=1)
    bh[...], bl[...] = split(right)
    th[...], tl[...] = split(right.T)

    @pl.when(core == 0)
    def _():
        pl.semaphore_wait(barrier, (slabs - 1) * 2 * RING)
        greet(ring_sem, 2 * slab + 1, bond)

    @pl.when(core == 1)
    def _():
        pl.semaphore_wait(ring_sem, 1)

    gate = gates[block, 2 * (ring % 2)]
    passed = []
    squares = None
    for d in range(GROUPS):
        g = grouped(bond // part, d)
        if d == 1:
            pass_on(0, 1)
            pass_on(0, 2)
        if d == 2:
            pass_on(0, 3)
        complete(0, d)
        left = jnp.concatenate([spin(0, s, g * tier, tier) for s in range(2)], axis=0)
        theta = times(split(left), (bh[...], bl[...]))
        matrix = split(mixed(theta, gate, width))
        here = pl.ds(d * 2 * tier, 2 * tier)
        mh[here, :], ml[here, :] = matrix
        projected = times(matrix, (th[...], tl[...]))
        for s in range(2):
            rsend[s, pl.ds(g * tier, tier)] = projected[s * tier:(s + 1) * tier]
        piece = pl.ds(g * tier, tier)
        copy = remote(
            rsend.at[core, piece], rrecv.at[core, piece], m_send.at[d], m_recv.at[d],
            2 * slab_to + core, prev_bond,
        )
        copy.start()
        passed.append(copy)
        square = sum_of_squares(projected)
        squares = square if squares is None else squares + square
        ph[:, here], pl_[:, here] = split(projected.T)

    turned = (ph[...], pl_[...])
    inverse = 1.0 / (squares + EPSILON)
    gram = times_transposed(turned, turned) * inverse
    root = jnp.sqrt(inverse)

    def carry_even(q):
        here = slice(q * width, (q + 1) * width)
        kept[:, here] = times(turned, (mh[:, here], ml[:, here])) * root

    factor = newton_schulz(gram, [functools.partial(carry_even, q) for q in range(2)])
    carried = times(factor, split(kept[...]))
    scale_norm = norm_of(carried)
    weight_even = jnp.log(scale_norm)
    carried = split(carried * (1.0 / scale_norm))
    for s in range(2):
        lh[s * width:(s + 1) * width, :] = carried[0][:, s * width:(s + 1) * width]
        ll[s * width:(s + 1) * width, :] = carried[1][:, s * width:(s + 1) * width]

    gram = None
    squares = None
    for d in range(GROUPS):
        piece = rrecv.at[core, pl.ds(grouped(next_bond // part, d) * tier, tier)]
        landed(piece, m_recv.at[d])
        copy = remote(piece, piece, h_send.at[d], h_recv.at[d], sibling["chain"], bond)
        copy.start()
        forwards.append(copy)
        if d % 2 == 0:
            continue
        parts = []
        for e in (d - 1, d):
            g = grouped(next_bond // part, e)
            landed(rrecv.at[1 - core, pl.ds(g * tier, tier)], h_recv.at[e])
            for s in range(2):
                parts.append(rrecv[s, pl.ds(g * tier, tier)])
        received = jnp.concatenate(parts, axis=0)
        square = sum_of_squares(received)
        squares = square if squares is None else squares + square
        turned = split(received.T)
        piece = split(received)
        for k, (e, s) in enumerate([(e, s) for e in (d - 1, d) for s in range(2)]):
            g = grouped(next_bond // part, e)
            nh[pl.ds(s * width + g * tier, tier), :] = piece[0][k * tier:(k + 1) * tier]
            nl[pl.ds(s * width + g * tier, tier), :] = piece[1][k * tier:(k + 1) * tier]
        product = times(turned, piece)
        gram = product if gram is None else gram + product
    inverse = 1.0 / (squares + EPSILON)
    gate = gates[block, 2 * (ring % 2) + 1]
    half = width // 2

    def ahead(q):
        left = tuple(
            jnp.concatenate([ref[s * width + q * half:s * width + (q + 1) * half, :] for s in range(2)], axis=0)
            for ref in (lh, ll)
        )
        theta = [times(left, (nh[t * width:(t + 1) * width, :], nl[t * width:(t + 1) * width, :])) for t in range(2)]
        here = slice(q * width, (q + 1) * width)
        uh[here, :], ul[here, :] = split(mixed(jnp.concatenate(theta, axis=1), gate, width))

    factor = newton_schulz(gram * inverse, [functools.partial(ahead, q) for q in range(2)])
    scale = math.sqrt(2 * width) * jnp.sqrt(inverse)
    for t in range(2):
        value = times((nh[t * width:(t + 1) * width, :], nl[t * width:(t + 1) * width, :]), factor) * scale
        bh[:, t * width:(t + 1) * width], bl[:, t * width:(t + 1) * width] = split(value)

    right = (bh[...], bl[...])
    squares = None
    for q in range(2):
        here = slice(q * width, (q + 1) * width)
        matrix = []
        for t in range(2):
            there = slice(t * width, (t + 1) * width)
            matrix.append(times((uh[here, there], ul[here, there]), factor) * scale)
        matrix = split(jnp.concatenate(matrix, axis=1))
        mh[here, :], ml[here, :] = matrix
        projected = times_transposed(matrix, right)
        square = sum_of_squares(projected)
        squares = square if squares is None else squares + square
        ph[:, here], pl_[:, here] = split(projected.T)
        piece = split(projected)
        for s in range(2):
            to = slice(s * width + q * half, s * width + (q + 1) * half)
            nh[to, :] = piece[0][s * half:(s + 1) * half]
            nl[to, :] = piece[1][s * half:(s + 1) * half]
    turned = (ph[...], pl_[...])
    inverse = 1.0 / (squares + EPSILON)
    gram = times_transposed(turned, turned) * inverse
    root = jnp.sqrt(inverse)

    def carry(q):
        here = slice(q * width, (q + 1) * width)
        kept[:, here] = times(turned, (mh[:, here], ml[:, here])) * root

    factor = newton_schulz(gram, [functools.partial(carry, q) for q in range(2)])

    outs = []

    def put(h):
        site = lax.rem(slab * 2 * RING + 2 * ring + 1 + h, 4 * chains)
        chain_to, slot = (site // 4, site % 4)
        for k in range(2):
            j = lax.rem(bond % RING // 2 + 1 + k, 2)
            bond_to = replica * RING + 2 * j + core
            src = obuf.at[h, pl.ds(bond_to * tall, tall)]
            dst = out_ref.at[pl.ds(slot * tall, tall)]
            copy = remote(src, dst, o_send.at[h, k], o_recv.at[slot], chain_to, bond_to)
            here = pltpu.make_async_copy(src, dst, o_recv.at[slot])
            mine = jnp.logical_and(chain_to == chain, bond_to == bond)
            outs.append((copy, mine))
            pl.when(mine)(here.start)
            pl.when(jnp.logical_not(mine))(copy.start)

    wanted = [(s, j) for j in range(2) for s in range(2)]
    picked = tuple(
        jnp.concatenate(
            [ref[pl.ds(s * width + (replica * RING + 2 * j + core) * rows, rows), :] for s, j in wanted], axis=0
        )
        for ref in (nh, nl)
    )
    value = times(picked, factor) * (math.sqrt(2 * width) * root)
    for k, (s, j) in enumerate(wanted):
        for t in range(2):
            at = (replica * RING + 2 * j + core) * tall + 2 * t + s
            obuf[0, pl.ds(at, rows, stride=4), :] = value[k * rows:(k + 1) * rows, t * LANES:(t + 1) * LANES]
    put(0)
    carried = times(factor, split(kept[...]))
    scale_norm = norm_of(carried)
    weight_odd = jnp.log(scale_norm)
    new_right = carried * (1.0 / scale_norm)

    row = lax.broadcasted_iota(jnp.int32, (8, LANES), 0)
    lane = lax.broadcasted_iota(jnp.int32, (8, LANES), 1)
    own = wall.at[slab * RING + ring]
    own[...] = jnp.where(row == 0, weight_even, weight_odd)
    weights = []
    for dz in range(slabs):
        for dk in range(RING):
            if dz == 0 and dk == 0:
                continue
            slab_at = lax.rem(slab + dz, slabs)
            bond_to = replica * RING + place_of(lax.rem(ring + dk, RING), slab_at)
            at = dz * RING + dk
            copy = remote(own, own, w_send.at[at], w_recv.at[at], 2 * slab_at + core, bond_to)
            copy.start()
            weights.append((copy, dz, dk))
    for s in range(2):
        for t in range(2):
            obuf[1, pl.ds(2 * t + s, width, stride=4), :] = new_right[:, s * width + t * LANES:s * width + (t + 1) * LANES]
    put(1)
    for copy, dz, dk in weights:
        source = lax.rem(slab + slabs - dz, slabs) * RING + lax.rem(ring + RING - dk, RING)
        landed(wall.at[source], w_recv.at[dz * RING + dk])
    total = jnp.zeros((8, LANES), jnp.float32)
    for e in range(slabs * RING):
        counted = jnp.logical_and(row < 2, 2 * e + row <= 4 * chain + lane)
        total = total + jnp.where(counted, wall[e], 0.0)
    running = jnp.sum(total, axis=0, keepdims=True) * (1.0 / (4 * chains))
    profile_ref[...] = jnp.broadcast_to(running, (8, LANES))

    for slot in range(4):
        landed(out_ref.at[pl.ds(slot * tall, tall)], o_recv.at[slot])
    for copy, mine in gathers:
        pl.when(jnp.logical_not(mine))(copy.wait_send)
    gate_copy.wait_send()
    for copy in forwards + passed + [c for c, dz, dk in weights]:
        copy.wait_send()
    for copy, mine in outs:
        pl.when(jnp.logical_not(mine))(copy.wait_send)


def per_device(chains, bonds, site_tensors, bond_gates):
    sites, rows, spins, width = site_tensors.shape
    assert sites == 4 and spins == 2 and width == 2 * LANES and bonds % RING == 0 and chains % 2 == 0
    cut = (sites, rows, spins, width // LANES, LANES)
    flat = site_tensors.reshape(cut).transpose(0, 1, 3, 2, 4).reshape(sites * rows * 4, LANES)
    slabs = chains // 2
    dma = pltpu.SemaphoreType.DMA
    wide, tall = ((width, 2 * width), (2 * width, width))
    half = [pltpu.VMEM(shape, jnp.bfloat16) for shape in (wide, wide, tall, tall, (2 * width, 2 * width), (2 * width, 2 * width), wide, wide, tall, tall, tall, tall, (2 * width, 2 * width), (2 * width, 2 * width))]
    out, profile = pl.pallas_call(
        functools.partial(kernel, chains, bonds, rows, width),
        out_shape=(
            jax.ShapeDtypeStruct(flat.shape, jnp.float32),
            jax.ShapeDtypeStruct((8, LANES), jnp.float32),
        ),
        in_specs=[pl.BlockSpec(memory_space=pltpu.HBM)] * 2,
        out_specs=(pl.BlockSpec(memory_space=pl.ANY), pl.BlockSpec(memory_space=pltpu.VMEM)),
        scratch_shapes=[
            pltpu.SemaphoreType.REGULAR,
            pltpu.SemaphoreType.REGULAR,
            dma,
            pltpu.VMEM(flat.shape, jnp.float32),
            pltpu.VMEM((2, 4 * width, LANES), jnp.float32),
            pltpu.VMEM((2,) + bond_gates.shape, jnp.float32),
            pltpu.VMEM((2, width, width), jnp.float32),
            pltpu.VMEM((2, width, width), jnp.float32),
            pltpu.VMEM((2, 4 * width, LANES), jnp.float32),
            pltpu.VMEM((slabs * RING, 8, LANES), jnp.float32),
            *half,
            pltpu.VMEM(wide, jnp.float32),
            dma((2, 2, 2, bonds // RING)), dma((2, bonds)),
            dma((2, bonds)), dma((2, bonds)),
            dma, dma((2,)),
            dma((GROUPS,)), dma((GROUPS,)),
            dma((GROUPS,)), dma((GROUPS,)),
            dma((2, 2)), dma((4,)),
            dma((slabs * RING,)), dma((slabs * RING,)),
        ],
        compiler_params=pltpu.CompilerParams(
            has_side_effects=True, collective_id=0, vmem_limit_bytes=56_000_000
        ),
    )(flat, bond_gates)
    cut = (sites, rows, width // LANES, spins, LANES)
    state = out.reshape(cut).transpose(0, 1, 3, 2, 4).reshape(site_tensors.shape)
    return (state, profile[0, :sites])


def solution(mesh):
    chains, bonds = (mesh.shape["chain"], mesh.shape["bond"])
    return jax.shard_map(
        functools.partial(per_device, chains, bonds),
        mesh=mesh,
        in_specs=(P("chain", "bond", None, None), P("chain", None, None)),
        out_specs=(P("chain", "bond", None, None), P("chain")),
        check_vma=False,
    )
```

time: 45.2 us -> 41.6 us (0.920)
  the two profiles are of different devices: /device:TPU:11 before, /device:TPU:0 now
where the time goes in v1:
time: 41.6 us; the launch traced here: 41.4 us
  Pallas kernels  38.8 us (93%)
  local copies, waits for them, and re-layouts  2 us (5%)
  between operations  0.65 us (2%)
    pallas_call x1, Pallas kernels, per_device(): pl.pallas_call(functools.partial(kernel, chains, bonds, rows, width), out...  38.8 us
    unnamed x3, local copies, waits for them, and re-layouts  1.48 us

profile of v1, /device:TPU:0, one launch (start us, length us, event | category | flops | bytes accessed | tf_op | source)
XLA Modules:
  0.0 41.4 jit_solution(8198052132588387820)
XLA Ops:
  0.6 0.0 copy-start
  0.6 0.7 %copy-done = f32[4,4,4]{2,1,0:T(4,128)S(1)} copy-done((f32[4,4,4]{2,1,0:T(4,128)S(1)}, f32[4,4,4]{2,1,0:T(4,128)}, u32[]{:S(2)}) %copy-start) | copy-done | bytes 280
  1.3 38.8 %shard_map.41 = (f32[1024,128]{1,0:T(8,128)S(1)}, f32[8,128]{1,0:T(8,128)S(1)}) custom-call(f32[1024,128]{1,0:T(8,128)} %bitcast.13, f32[4,4,4]{2,1,0:T(4,128)S(1)} %copy-done), custom_call_target="tpu_custom_call" | custom-call | tf_op jit(solution)/shard_map/pallas_call | solution.py:455
  40.1 0.5 %slice_bitcast_fusion = f32[4]{0:T(128)} fusion(f32[8,128]{1,0:T(8,128)S(1)} %get-tuple-element.5), kind=kLoop, calls=%fused_computation | loop fusion | bytes 32 | tf_op jit(solution)/shard_map/squeeze | solution.py:490
  40.6 0.8 %copy.7 = f32[4,64,2,256]{3,2,1,0:T(2,128)} copy(f32[4,64,2,256]{3,2,1,0:T(2,128)S(1)} %bitcast.12) | data formatting | bytes 1048576
Async XLA Ops:
  0.6 0.7 %copy-start = (f32[4,4,4]{2,1,0:T(4,128)S(1)}, f32[4,4,4]{2,1,0:T(4,128)}, u32[]{:S(2)}) copy-start(f32[4,4,4]{2,1,0:T(4,128)} %gates_ref.1) | copy-start | bytes 772

commit v2 on v0

v2 whole, which is shorter than its diff:
```python
import functools
import math

import jax
import jax.numpy as jnp
from jax import lax
from jax.experimental import pallas as pl
from jax.experimental.pallas import tpu as pltpu
from jax.sharding import PartitionSpec as P

NS_ITERS = 3
RING = 4
GROUPS = 4
LANES = 128
EPSILON = 1e-06


def split(value):
    high = value.astype(jnp.bfloat16)
    low = (value - high.astype(jnp.float32)).astype(jnp.bfloat16)
    return (high, low)


def dot(a, b):
    return jnp.dot(a, b, preferred_element_type=jnp.float32)


def dot_t(a, b):
    return lax.dot_general(a, b, (((1,), (1,)), ((), ())), preferred_element_type=jnp.float32)


def times(a, b):
    (ah, al), (bh, bl) = (a, b)
    return dot(ah, bh) + dot(al, bh) + dot(ah, bl)


def times_transposed(a, b):
    (ah, al), (bh, bl) = (a, b)
    return dot_t(ah, bh) + dot_t(al, bh) + dot_t(ah, bl)


def mixed(theta, gate, width):
    r = theta.shape[0] // 2
    theta = [[theta[u * r:(u + 1) * r, v * width:(v + 1) * width] for v in range(2)] for u in range(2)]
    scaled = gate * (1.0 / math.sqrt(width))
    rows = []
    for s in range(2):
        row = []
        for t in range(2):
            total = None
            for u in range(2):
                for v in range(2):
                    factor = scaled[2 * s + t:2 * s + t + 1, 2 * u + v:2 * u + v + 1]
                    term = factor * theta[u][v]
                    total = term if total is None else total + term
            row.append(total)
        rows.append(jnp.concatenate(row, axis=1))
    return jnp.concatenate(rows, axis=0)


def newton_schulz(gram, fill=()):
    assert NS_ITERS == 3
    fill = list(fill)

    def filled(value):
        if fill:
            fill.pop(0)()
        return value

    eye = jnp.where(
        lax.broadcasted_iota(jnp.int32, gram.shape, 0) == lax.broadcasted_iota(jnp.int32, gram.shape, 1),
        jnp.float32(1.5),
        jnp.float32(0.0),
    )
    factor = None
    for repeat in range(NS_ITERS):
        step = eye - 0.5 * gram
        factor = step if factor is None else times(split(factor), split(step))
        if repeat < NS_ITERS - 1:
            gram_split = split(gram)
            once = 1.5 * gram - 0.5 * filled(times(gram_split, gram_split))
            gram = 1.5 * once - 0.5 * filled(times(split(once), gram_split))
    while fill:
        fill.pop(0)()
    return split(factor)


def sum_of_squares(value):
    return jnp.sum(value * value, keepdims=True)


def norm_of(carried):
    mean = sum_of_squares(carried) * (1.0 / carried.size)
    return jnp.sqrt(mean + EPSILON)


def order(place):
    return place + (place // 2) * (1 - 2 * (place % 2))


def grouped(mine, d):
    if d == 0:
        return mine
    if d == 1:
        return mine + 1 - 2 * (mine % 2)
    if d == 2:
        return lax.rem(mine + 2, 4)
    return 3 - mine


def kernel(
    chains, bonds, rows, width,
    x_ref, gates_ref, out_ref, profile_ref,
    slab_sem, ring_sem, fetch_sem, xin, inbuf, gates, rsend, rrecv, obuf, wall, below,
    bh, bl, th, tl, mh, ml, ph, pl_, lh, ll, nh, nl, uh, ul, kept,
    g_send, g_recv, gate_send, gate_recv,
    m_send, m_recv, o_send, o_recv, w_send, w_recv, p_send, p_recv,
):
    chain, bond = (lax.axis_index("chain"), lax.axis_index("bond"))
    slabs = chains // 2
    slab, core = (chain // 2, chain % 2)
    tall = rows * 4
    part = bonds // GROUPS
    tier = width // GROUPS
    half = width // 2
    replica = bond // RING
    ring = order(bond % RING)
    block = ring // 2

    def on(which):
        return pl.when(core == which)

    def at(slab_at, core_at, bond_at):
        return {"chain": 2 * slab_at + core_at, "bond": bond_at}

    def remote(src, dst, send, recv_sem, to):
        return pltpu.make_async_remote_copy(
            src_ref=src, dst_ref=dst, send_sem=send, recv_sem=recv_sem,
            device_id=to, device_id_type=pl.DeviceIdType.MESH,
        )

    def landed(ref, sem):
        pltpu.make_async_copy(ref, ref, sem).wait()

    def greet(semaphore, to):
        pl.semaphore_signal(semaphore, inc=1, device_id=to, device_id_type=pl.DeviceIdType.MESH)

    fetch = pltpu.make_async_copy(x_ref, xin, fetch_sem)
    fetch.start()
    gate_here = pltpu.make_async_copy(gates_ref, gates.at[1], gate_recv.at[1])
    gate_copy = remote(gates_ref, gates.at[0], gate_send, gate_recv.at[0], at(slab, 1, bond))
    barrier = pltpu.get_barrier_semaphore()

    @on(1)
    def _():
        gate_here.start()
        for db in range(1, bonds):
            greet(barrier, at(slab, 1, lax.rem(bond + db, bonds)))

    @on(0)
    def _():
        greet(barrier, at(slab, 1, bond))
        for db in range(1, RING):
            greet(barrier, at(slab, 0, replica * RING + lax.rem(bond + db, RING)))

    for dz in range(1, slabs):
        for db in range(RING):
            greet(barrier, at(lax.rem(slab + dz, slabs), 0, replica * RING + lax.rem(bond + db, RING)))

    @on(1)
    def _():
        pl.semaphore_wait(barrier, bonds)
        greet(slab_sem, at(slab, 0, bond))

    @on(0)
    def _():
        pl.semaphore_wait(slab_sem, 1)

    fetch.wait()
    gathers = []
    for i in (1, 0):
        for j in range(2):
            for r in range(bonds // RING):
                bond_to = r * RING + order(2 * core + j)
                src = xin.at[pl.ds((2 * j + i) * tall, tall)]
                dst = inbuf.at[i, pl.ds(bond * tall, tall)]
                sem = g_recv.at[i, bond]
                copy = remote(src, dst, g_send.at[i, j, r], sem, at(slab, 1, bond_to))
                here = pltpu.make_async_copy(src, dst, sem)
                mine = jnp.logical_and(core == 1, bond_to == bond)
                gathers.append((copy, here, mine))
                pl.when(jnp.logical_not(mine))(copy.start)
    for copy, here, mine in gathers:
        pl.when(mine)(here.start)

    def gathers_sent():
        for copy, here, mine in gathers:
            pl.when(jnp.logical_not(mine))(copy.wait_send)

    def outputs_landed():
        for slot in range(4):
            landed(out_ref.at[pl.ds(slot * tall, tall)], o_recv.at[slot])

    @on(0)
    def _():
        gate_copy.start()
        pl.semaphore_wait(barrier, RING - 1 + (slabs - 1) * 2 * RING)
        greet(ring_sem, at(slab, 1, bond))
        gathers_sent()
        gate_copy.wait_send()
        outputs_landed()
        landed(profile_ref, p_recv)

    def gathered(i, d):
        for e in range(part):
            origin = grouped(bond // part, d) * part + lax.rem(bond + e, part)
            landed(inbuf.at[i, pl.ds(origin * tall, tall)], g_recv.at[i, origin])

    def spin(i, s, row, count):
        return jnp.concatenate(
            [inbuf[i, pl.ds(4 * row + 2 * t + s, count, stride=4), :] for t in range(2)], axis=1
        )

    @on(1)
    def _():
        before = lax.rem(ring + RING - 1, RING)
        slab_to = lax.rem(slab + slabs - jnp.where(ring == 0, 1, 0), slabs)
        previous = at(slab_to, 1, replica * RING + order(before))
        next_bond = replica * RING + order(lax.rem(ring + 1, RING))

        for d in range(GROUPS):
            gathered(1, d)
        landed(gates.at[0], gate_recv.at[0])
        landed(gates.at[1], gate_recv.at[1])
        right = jnp.concatenate([spin(1, s, 0, width) for s in range(2)], axis=1)
        bh[...], bl[...] = split(right)
        th[...], tl[...] = split(right.T)
        pl.semaphore_wait(ring_sem, 1)

        gate = gates[block, 2 * (ring % 2)]
        passed = []
        squares = None
        for d in range(GROUPS):
            g = grouped(bond // part, d)
            gathered(0, d)
            left = jnp.concatenate([spin(0, s, g * tier, tier) for s in range(2)], axis=0)
            theta = times(split(left), (bh[...], bl[...]))
            matrix = split(mixed(theta, gate, width))
            here = pl.ds(d * 2 * tier, 2 * tier)
            mh[here, :], ml[here, :] = matrix
            projected = times(matrix, (th[...], tl[...]))
            piece = pl.ds(g * 2 * tier, 2 * tier)
            rsend[piece, :] = projected
            copy = remote(rsend.at[piece], rrecv.at[piece], m_send.at[d], m_recv.at[d], previous)
            copy.start()
            passed.append(copy)
            square = sum_of_squares(projected)
            squares = square if squares is None else squares + square
            ph[:, here], pl_[:, here] = split(projected.T)

        turned = (ph[...], pl_[...])
        inverse = 1.0 / (squares + EPSILON)
        gram = times_transposed(turned, turned) * inverse
        root = jnp.sqrt(inverse)

        def carry_even(q):
            here = slice(q * width, (q + 1) * width)
            kept[:, here] = times(turned, (mh[:, here], ml[:, here])) * root

        factor = newton_schulz(gram, [functools.partial(carry_even, q) for q in range(2)])
        carried = times(factor, split(kept[...]))
        scale_norm = norm_of(carried)
        weight_even = jnp.log(scale_norm)
        carried = split(carried * (1.0 / scale_norm))
        for s in range(2):
            lh[s * width:(s + 1) * width, :] = carried[0][:, s * width:(s + 1) * width]
            ll[s * width:(s + 1) * width, :] = carried[1][:, s * width:(s + 1) * width]

        gram = None
        squares = None
        for d in range(1, GROUPS, 2):
            parts = []
            for e in (d - 1, d):
                g = grouped(next_bond // part, e)
                piece = pl.ds(g * 2 * tier, 2 * tier)
                landed(rrecv.at[piece], m_recv.at[e])
                parts.append(rrecv[piece, :])
            received = jnp.concatenate(parts, axis=0)
            square = sum_of_squares(received)
            squares = square if squares is None else squares + square
            turned = split(received.T)
            piece = split(received)
            for k, (e, s) in enumerate([(e, s) for e in (d - 1, d) for s in range(2)]):
                g = grouped(next_bond // part, e)
                nh[pl.ds(s * width + g * tier, tier), :] = piece[0][k * tier:(k + 1) * tier]
                nl[pl.ds(s * width + g * tier, tier), :] = piece[1][k * tier:(k + 1) * tier]
            product = times(turned, piece)
            gram = product if gram is None else gram + product
        inverse = 1.0 / (squares + EPSILON)
        gate = gates[block, 2 * (ring % 2) + 1]

        def ahead(q):
            left = tuple(
                jnp.concatenate([ref[s * width + q * half:s * width + (q + 1) * half, :] for s in range(2)], axis=0)
                for ref in (lh, ll)
            )
            theta = [times(left, (nh[t * width:(t + 1) * width, :], nl[t * width:(t + 1) * width, :])) for t in range(2)]
            here = slice(q * width, (q + 1) * width)
            uh[here, :], ul[here, :] = split(mixed(jnp.concatenate(theta, axis=1), gate, width))

        factor = newton_schulz(gram * inverse, [functools.partial(ahead, q) for q in range(2)])
        scale = math.sqrt(2 * width) * jnp.sqrt(inverse)
        for t in range(2):
            value = times((nh[t * width:(t + 1) * width, :], nl[t * width:(t + 1) * width, :]), factor) * scale
            bh[:, t * width:(t + 1) * width], bl[:, t * width:(t + 1) * width] = split(value)

        right = (bh[...], bl[...])
        squares = None
        for q in range(2):
            here = slice(q * width, (q + 1) * width)
            matrix = []
            for t in range(2):
                there = slice(t * width, (t + 1) * width)
                matrix.append(times((uh[here, there], ul[here, there]), factor) * scale)
            matrix = split(jnp.concatenate(matrix, axis=1))
            mh[here, :], ml[here, :] = matrix
            projected = times_transposed(matrix, right)
            square = sum_of_squares(projected)
            squares = square if squares is None else squares + square
            ph[:, here], pl_[:, here] = split(projected.T)
            piece = split(projected)
            for s in range(2):
                to = slice(s * width + q * half, s * width + (q + 1) * half)
                nh[to, :] = piece[0][s * half:(s + 1) * half]
                nl[to, :] = piece[1][s * half:(s + 1) * half]
        turned = (ph[...], pl_[...])
        inverse = 1.0 / (squares + EPSILON)
        gram = times_transposed(turned, turned) * inverse
        root = jnp.sqrt(inverse)

        def carry(q):
            here = slice(q * width, (q + 1) * width)
            kept[:, here] = times(turned, (mh[:, here], ml[:, here])) * root

        factor = newton_schulz(gram, [functools.partial(carry, q) for q in range(2)])
        outs = []

        def put(h):
            site = lax.rem(slab * 2 * RING + 2 * ring + 1 + h, 4 * chains)
            chain_to, slot = (site // 4, site % 4)
            for k in range(RING):
                bond_to = replica * RING + grouped(bond % RING, RING - 1 - k)
                src = obuf.at[h, pl.ds(bond_to * tall, tall)]
                dst = out_ref.at[pl.ds(slot * tall, tall)]
                copy = remote(src, dst, o_send.at[h, k], o_recv.at[slot], {"chain": chain_to, "bond": bond_to})
                if k < RING - 1:
                    copy.start()
                    outs.append((copy, None))
                    continue
                here = pltpu.make_async_copy(src, dst, o_recv.at[slot])
                mine = chain_to == chain
                outs.append((copy, mine))
                pl.when(mine)(here.start)
                pl.when(jnp.logical_not(mine))(copy.start)

        carried = times(factor, split(kept[...]))
        scale_norm = norm_of(carried)
        weight_odd = jnp.log(scale_norm)
        new_right = carried * (1.0 / scale_norm)

        row = lax.broadcasted_iota(jnp.int32, (8, LANES), 0)
        lane = lax.broadcasted_iota(jnp.int32, (8, LANES), 1)
        own = wall.at[slab * RING + ring]
        own[...] = jnp.where(row == 0, weight_even, weight_odd)
        weights = []
        for dz in range(slabs):
            for dk in range(RING):
                if dz == 0 and dk == 0:
                    continue
                to = at(lax.rem(slab + dz, slabs), 1, replica * RING + order(lax.rem(ring + dk, RING)))
                k = dz * RING + dk
                copy = remote(own, own, w_send.at[k], w_recv.at[k], to)
                copy.start()
                weights.append((copy, dz, dk))
        for s in range(2):
            for t in range(2):
                obuf[1, pl.ds(2 * t + s, width, stride=4), :] = (
                    new_right[:, s * width + t * LANES:s * width + (t + 1) * LANES]
                )
        put(1)
        value = times((nh[...], nl[...]), factor) * (math.sqrt(2 * width) * root)
        for s in range(2):
            for t in range(2):
                obuf[0, pl.ds(2 * t + s, width, stride=4), :] = (
                    value[s * width:(s + 1) * width, t * LANES:(t + 1) * LANES]
                )
        put(0)

        for copy, dz, dk in weights:
            source = lax.rem(slab + slabs - dz, slabs) * RING + lax.rem(ring + RING - dk, RING)
            landed(wall.at[source], w_recv.at[dz * RING + dk])
        totals = [jnp.zeros((8, LANES), jnp.float32) for _ in range(2)]
        for e in range(slabs * RING):
            for c in range(2):
                counted = jnp.logical_and(row < 2, 2 * e + row <= 4 * (2 * slab + c) + lane)
                totals[c] = totals[c] + jnp.where(counted, wall[e], 0.0)
        running = [
            jnp.broadcast_to(jnp.sum(total, axis=0, keepdims=True) * (1.0 / (4 * chains)), (8, LANES))
            for total in totals
        ]
        below[...] = running[0]
        profile_ref[...] = running[1]
        lower = remote(below, profile_ref, p_send, p_recv, at(slab, 0, bond))
        lower.start()

        outputs_landed()
        gathers_sent()
        for copy in passed + [c for c, dz, dk in weights] + [lower]:
            copy.wait_send()
        for copy, mine in outs:
            if mine is None:
                copy.wait_send()
            else:
                pl.when(jnp.logical_not(mine))(copy.wait_send)


def per_device(chains, bonds, site_tensors, bond_gates):
    sites, rows, spins, width = site_tensors.shape
    assert sites == 4 and spins == 2 and width == 2 * LANES and bonds % RING == 0 and chains % 2 == 0
    cut = (sites, rows, spins, width // LANES, LANES)
    flat = site_tensors.reshape(cut).transpose(0, 1, 3, 2, 4).reshape(sites * rows * 4, LANES)
    slabs = chains // 2
    dma = pltpu.SemaphoreType.DMA
    wide, tall = ((width, 2 * width), (2 * width, width))
    half = [pltpu.VMEM(shape, jnp.bfloat16) for shape in (wide, wide, tall, tall, (2 * width, 2 * width), (2 * width, 2 * width), wide, wide, tall, tall, tall, tall, (2 * width, 2 * width), (2 * width, 2 * width))]
    out, profile = pl.pallas_call(
        functools.partial(kernel, chains, bonds, rows, width),
        out_shape=(
            jax.ShapeDtypeStruct(flat.shape, jnp.float32),
            jax.ShapeDtypeStruct((8, LANES), jnp.float32),
        ),
        in_specs=[pl.BlockSpec(memory_space=pltpu.HBM)] * 2,
        out_specs=(pl.BlockSpec(memory_space=pl.ANY), pl.BlockSpec(memory_space=pltpu.VMEM)),
        scratch_shapes=[
            pltpu.SemaphoreType.REGULAR,
            pltpu.SemaphoreType.REGULAR,
            dma,
            pltpu.VMEM(flat.shape, jnp.float32),
            pltpu.VMEM((2, 4 * width, LANES), jnp.float32),
            pltpu.VMEM((2,) + bond_gates.shape, jnp.float32),
            pltpu.VMEM((2 * width, width), jnp.float32),
            pltpu.VMEM((2 * width, width), jnp.float32),
            pltpu.VMEM((2, 4 * width, LANES), jnp.float32),
            pltpu.VMEM((slabs * RING, 8, LANES), jnp.float32),
            pltpu.VMEM((8, LANES), jnp.float32),
            *half,
            pltpu.VMEM(wide, jnp.float32),
            dma((2, 2, bonds // RING)), dma((2, bonds)),
            dma, dma((2,)),
            dma((GROUPS,)), dma((GROUPS,)),
            dma((2, RING)), dma((4,)),
            dma((slabs * RING,)), dma((slabs * RING,)),
            dma, dma,
        ],
        compiler_params=pltpu.CompilerParams(
            has_side_effects=True, collective_id=0, vmem_limit_bytes=56_000_000
        ),
    )(flat, bond_gates)
    cut = (sites, rows, width // LANES, spins, LANES)
    state = out.reshape(cut).transpose(0, 1, 3, 2, 4).reshape(site_tensors.shape)
    return (state, profile[0, :sites])


def solution(mesh):
    chains, bonds = (mesh.shape["chain"], mesh.shape["bond"])
    return jax.shard_map(
        functools.partial(per_device, chains, bonds),
        mesh=mesh,
        in_specs=(P("chain", "bond", None, None), P("chain", None, None)),
        out_specs=(P("chain", "bond", None, None), P("chain")),
        check_vma=False,
    )
```

time: 45.2 us -> 36.4 us (0.81)
  Pallas kernels: 42.4 us -> 33.6 us
    pallas_call x1, Pallas kernels: 42.4 us -> 33.6 us  [per_device(): pl.pallas_call(functools.partial(kernel, chains, bonds, rows, width), out...]
where the time goes in v2:
time: 36.4 us; the launch traced here: 36.2 us
  Pallas kernels  33.6 us (92%)
  local copies, waits for them, and re-layouts  2 us (5%)
  between operations  0.65 us (2%)
    pallas_call x1, Pallas kernels, per_device(): pl.pallas_call(functools.partial(kernel, chains, bonds, rows, width), out...  33.6 us
    unnamed x3, local copies, waits for them, and re-layouts  1.48 us

profile of v2, /device:TPU:11, one launch (start us, length us, event | category | flops | bytes accessed | tf_op | source)
XLA Modules:
  0.0 36.2 jit_solution(8690444905297919351)
XLA Ops:
  0.6 0.0 copy-start
  0.6 0.7 %copy-done = f32[4,4,4]{2,1,0:T(4,128)S(1)} copy-done((f32[4,4,4]{2,1,0:T(4,128)S(1)}, f32[4,4,4]{2,1,0:T(4,128)}, u32[]{:S(2)}) %copy-start) | copy-done | bytes 280
  1.3 33.6 %shard_map.41 = (f32[1024,128]{1,0:T(8,128)S(1)}, f32[8,128]{1,0:T(8,128)S(1)}) custom-call(f32[1024,128]{1,0:T(8,128)} %bitcast.13, f32[4,4,4]{2,1,0:T(4,128)S(1)} %copy-done), custom_call_target="tpu_custom_call" | custom-call | tf_op jit(solution)/shard_map/pallas_call | solution.py:436
  34.9 0.5 %slice_bitcast_fusion = f32[4]{0:T(128)} fusion(f32[8,128]{1,0:T(8,128)S(1)} %get-tuple-element.5), kind=kLoop, calls=%fused_computation | loop fusion | bytes 32 | tf_op jit(solution)/shard_map/squeeze | solution.py:471
  35.4 0.8 %copy.7 = f32[4,64,2,256]{3,2,1,0:T(2,128)} copy(f32[4,64,2,256]{3,2,1,0:T(2,128)S(1)} %bitcast.12) | data formatting | bytes 1048576
Async XLA Ops:
  0.6 0.7 %copy-start = (f32[4,4,4]{2,1,0:T(4,128)S(1)}, f32[4,4,4]{2,1,0:T(4,128)}, u32[]{:S(2)}) copy-start(f32[4,4,4]{2,1,0:T(4,128)} %gates_ref.1) | copy-start | bytes 772

commit v3 on v2

--- a/solution.py
+++ b/solution.py
@@ -11,6 +11,7 @@
 NS_ITERS = 3
 RING = 4
 GROUPS = 4
+PIECES = 1
 LANES = 128
 EPSILON = 1e-06
 
@@ -368,10 +369,10 @@
         weight_odd = jnp.log(scale_norm)
         new_right = carried * (1.0 / scale_norm)
 
-        row = lax.broadcasted_iota(jnp.int32, (8, LANES), 0)
-        lane = lax.broadcasted_iota(jnp.int32, (8, LANES), 1)
+        lane = lax.broadcasted_iota(jnp.int32, (1, LANES), 1)
+        odd = lane // (LANES // 2)
         own = wall.at[slab * RING + ring]
-        own[...] = jnp.where(row == 0, weight_even, weight_odd)
+        own[...] = jnp.where(odd == 0, weight_even, weight_odd)
         weights = []
         for dz in range(slabs):
             for dk in range(RING):
@@ -380,7 +381,7 @@
                 to = at(lax.rem(slab + dz, slabs), 1, replica * RING + order(lax.rem(ring + dk, RING)))
                 k = dz * RING + dk
                 copy = remote(own, own, w_send.at[k], w_recv.at[k], to)
-                copy.start()
+                pl.when(slab + dz < slabs)(copy.start)
                 weights.append((copy, dz, dk))
         for s in range(2):
             for t in range(2):
@@ -398,14 +399,17 @@
 
         for copy, dz, dk in weights:
             source = lax.rem(slab + slabs - dz, slabs) * RING + lax.rem(ring + RING - dk, RING)
-            landed(wall.at[source], w_recv.at[dz * RING + dk])
-        totals = [jnp.zeros((8, LANES), jnp.float32) for _ in range(2)]
+
+            @pl.when(slab >= dz)
+            def _():
+                landed(wall.at[source], w_recv.at[dz * RING + dk])
+        totals = [jnp.zeros((1, LANES), jnp.float32) for _ in range(2)]
         for e in range(slabs * RING):
             for c in range(2):
-                counted = jnp.logical_and(row < 2, 2 * e + row <= 4 * (2 * slab + c) + lane)
+                counted = 2 * e + odd <= 4 * (2 * slab + c) + lane % (LANES // 2)
                 totals[c] = totals[c] + jnp.where(counted, wall[e], 0.0)
         running = [
-            jnp.broadcast_to(jnp.sum(total, axis=0, keepdims=True) * (1.0 / (4 * chains)), (8, LANES))
+            jnp.broadcast_to((total + pltpu.roll(total, LANES // 2, 1)) * (1.0 / (4 * chains)), (8, LANES))
             for total in totals
         ]
         below[...] = running[0]
@@ -415,13 +419,31 @@
 
         outputs_landed()
         gathers_sent()
-        for copy in passed + [c for c, dz, dk in weights] + [lower]:
+        for copy in passed + [lower]:
             copy.wait_send()
+        for copy, dz, dk in weights:
+            pl.when(slab + dz < slabs)(copy.wait_send)
         for copy, mine in outs:
             if mine is None:
                 copy.wait_send()
             else:
                 pl.when(jnp.logical_not(mine))(copy.wait_send)
+
+
+def finish(out_ref, weights_ref, state_ref, profile_ref, held, state_sem, profile_sem):
+    held[...] = weights_ref[0, :held.shape[0]]
+    last = pltpu.make_async_copy(held, profile_ref, profile_sem)
+    last.start()
+    size = out_ref.shape[0] // PIECES
+    copies = []
+    for k in range(PIECES):
+        here = pl.ds(k * size, size)
+        copy = pltpu.make_async_copy(out_ref.at[here], state_ref.at[here], state_sem.at[k])
+        copy.start()
+        copies.append(copy)
+    for copy in copies:
+        copy.wait()
+    last.wait()
 
 
 def per_device(chains, bonds, site_tensors, bond_gates):
@@ -451,7 +473,7 @@
             pltpu.VMEM((2 * width, width), jnp.float32),
             pltpu.VMEM((2 * width, width), jnp.float32),
             pltpu.VMEM((2, 4 * width, LANES), jnp.float32),
-            pltpu.VMEM((slabs * RING, 8, LANES), jnp.float32),
+            pltpu.VMEM((slabs * RING, 1, LANES), jnp.float32),
             pltpu.VMEM((8, LANES), jnp.float32),
             *half,
             pltpu.VMEM(wide, jnp.float32),
@@ -465,10 +487,21 @@
         compiler_params=pltpu.CompilerParams(
             has_side_effects=True, collective_id=0, vmem_limit_bytes=56_000_000
         ),
-    )(flat, bond_gates)
+    )(flat, pltpu.with_memory_space_constraint(bond_gates, pltpu.HBM))
+    out, profile = pl.pallas_call(
+        finish,
+        out_shape=(
+            jax.ShapeDtypeStruct(flat.shape, jnp.float32),
+            jax.ShapeDtypeStruct((sites,), jnp.float32),
+        ),
+        in_specs=[pl.BlockSpec(memory_space=pltpu.VMEM)] * 2,
+        out_specs=(pl.BlockSpec(memory_space=pl.ANY), pl.BlockSpec(memory_space=pl.ANY)),
+        scratch_shapes=[pltpu.VMEM((sites,), jnp.float32), pltpu.SemaphoreType.DMA((PIECES,)), pltpu.SemaphoreType.DMA],
+        compiler_params=pltpu.CompilerParams(vmem_limit_bytes=2_000_000),
+    )(out, profile)
     cut = (sites, rows, width // LANES, spins, LANES)
     state = out.reshape(cut).transpose(0, 1, 3, 2, 4).reshape(site_tensors.shape)
-    return (state, profile[0, :sites])
+    return (state, profile)
 
 
 def solution(mesh):

time: 36.4 us -> 34.1 us (0.937)
  the two profiles are of different devices: /device:TPU:11 before, /device:TPU:0 now
where the time goes in v3:
time: 34.1 us; the launch traced here: 33.6 us
  Pallas kernels  33 us (97%)
  between operations  0.64 us (2%)
    pallas_call x1, Pallas kernels, per_device(): pl.pallas_call(functools.partial(kernel, chains, bonds, rows, width), out...  32.2 us
    pallas_call x1, Pallas kernels, per_device(): pl.pallas_call(finish, out_shape=(jax.ShapeDtypeStruct(flat.shape, jnp.fl...  0.81 us

profile of v3, /device:TPU:0, one launch (start us, length us, event | category | flops | bytes accessed | tf_op | source)
XLA Modules:
  0.0 33.6 jit_solution(9143650580134765214)
XLA Ops:
  0.6 32.2 %shard_map.41 = (f32[1024,128]{1,0:T(8,128)S(1)}, f32[8,128]{1,0:T(8,128)S(1)}) custom-call(f32[1024,128]{1,0:T(8,128)} %bitcast.10, f32[4,4,4]{2,1,0:T(4,128)} %gates_ref.1), custom_call_target="tpu_custom_call" | custom-call | tf_op jit(solution)/shard_map/pallas_call | solution.py:458
  32.8 0.8 %shard_map.42 = (f32[1024,128]{1,0:T(8,128)}, f32[4]{0:T(128)}) custom-call(f32[1024,128]{1,0:T(8,128)S(1)} %get-tuple-element.6.out_ref, f32[8,128]{1,0:T(8,128)S(1)} %get-tuple-element.7.weights_ref), custom_call_target="tpu_custom_call" | custom-call | tf_op jit(solution)/shard_map/pallas_call | solution.py:491

commit v4 on v3

--- a/solution.py
+++ b/solution.py
@@ -116,6 +116,7 @@
     bh, bl, th, tl, mh, ml, ph, pl_, lh, ll, nh, nl, uh, ul, kept,
     g_send, g_recv, gate_send, gate_recv,
     m_send, m_recv, o_send, o_recv, w_send, w_recv, p_send, p_recv,
+    held, turn, d_send, d_recv, e_send, t_send, t_recv, u_send,
 ):
     chain, bond = (lax.axis_index("chain"), lax.axis_index("bond"))
     slabs = chains // 2
@@ -265,10 +266,11 @@
         root = jnp.sqrt(inverse)
 
         def carry_even(q):
-            here = slice(q * width, (q + 1) * width)
-            kept[:, here] = times(turned, (mh[:, here], ml[:, here])) * root
-
-        factor = newton_schulz(gram, [functools.partial(carry_even, q) for q in range(2)])
+            here = slice(q // 2 * width, (q // 2 + 1) * width)
+            there = slice(q % 2 * half, (q % 2 + 1) * half)
+            kept[there, here] = times((ph[there, :], pl_[there, :]), (mh[:, here], ml[:, here])) * root
+
+        factor = newton_schulz(gram, [functools.partial(carry_even, q) for q in range(4)])
         carried = times(factor, split(kept[...]))
         scale_norm = norm_of(carried)
         weight_even = jnp.log(scale_norm)
@@ -302,14 +304,16 @@
 
         def ahead(q):
             left = tuple(
-                jnp.concatenate([ref[s * width + q * half:s * width + (q + 1) * half, :] for s in range(2)], axis=0)
+                jnp.concatenate([ref[s * width + q * tier:s * width + (q + 1) * tier, :] for s in range(2)], axis=0)
                 for ref in (lh, ll)
             )
             theta = [times(left, (nh[t * width:(t + 1) * width, :], nl[t * width:(t + 1) * width, :])) for t in range(2)]
-            here = slice(q * width, (q + 1) * width)
-            uh[here, :], ul[here, :] = split(mixed(jnp.concatenate(theta, axis=1), gate, width))
-
-        factor = newton_schulz(gram * inverse, [functools.partial(ahead, q) for q in range(2)])
+            value = split(mixed(jnp.concatenate(theta, axis=1), gate, width))
+            for s in range(2):
+                here = slice(q // 2 * width + s * half + q % 2 * tier, q // 2 * width + s * half + (q % 2 + 1) * tier)
+                uh[here, :], ul[here, :] = (part[s * tier:(s + 1) * tier] for part in value)
+
+        factor = newton_schulz(gram * inverse, [functools.partial(ahead, q) for q in range(4)])
         scale = math.sqrt(2 * width) * jnp.sqrt(inverse)
         for t in range(2):
             value = times((nh[t * width:(t + 1) * width, :], nl[t * width:(t + 1) * width, :]), factor) * scale
@@ -340,30 +344,77 @@
         root = jnp.sqrt(inverse)
 
         def carry(q):
-            here = slice(q * width, (q + 1) * width)
-            kept[:, here] = times(turned, (mh[:, here], ml[:, here])) * root
-
-        factor = newton_schulz(gram, [functools.partial(carry, q) for q in range(2)])
-        outs = []
-
-        def put(h):
+            here = slice(q // 2 * width, (q // 2 + 1) * width)
+            there = slice(q % 2 * half, (q % 2 + 1) * half)
+            kept[there, here] = times((ph[there, :], pl_[there, :]), (mh[:, here], ml[:, here])) * root
+
+        factor = newton_schulz(gram, [functools.partial(carry, q) for q in range(4)])
+
+        crossing = ring == RING - 1
+        across, opposite = (grouped(bond % RING, d) for d in (1, 3))
+        swapped = ring % 2
+        targets = [
+            grouped(bond % RING, 2),
+            opposite + swapped * (1 - crossing.astype(jnp.int32)) * (across - opposite),
+            across + swapped * (1 - crossing.astype(jnp.int32)) * (opposite - across),
+            bond % RING,
+        ]
+        beside = replica * RING + grouped(bond % RING, 1)
+        short = tall // 2
+        detours = [
+            remote(
+                obuf.at[1, pl.ds(beside * tall + c * short, short)], held.at[pl.ds(c * short, short)],
+                d_send.at[c], d_recv.at[c], at(slab, 1, beside),
+            )
+            for c in range(2)
+        ]
+        relaying = ring == RING - 2
+        relays = [
+            remote(
+                held.at[pl.ds(c * short, short)], out_ref.at[pl.ds(c * short, short)],
+                e_send.at[c], o_recv.at[0], at(lax.rem(slab + 1, slabs), 0, bond),
+            )
+            for c in range(2)
+        ]
+
+        def output(h):
             site = lax.rem(slab * 2 * RING + 2 * ring + 1 + h, 4 * chains)
             chain_to, slot = (site // 4, site % 4)
+            made = []
             for k in range(RING):
-                bond_to = replica * RING + grouped(bond % RING, RING - 1 - k)
+                bond_to = replica * RING + targets[k]
                 src = obuf.at[h, pl.ds(bond_to * tall, tall)]
                 dst = out_ref.at[pl.ds(slot * tall, tall)]
                 copy = remote(src, dst, o_send.at[h, k], o_recv.at[slot], {"chain": chain_to, "bond": bond_to})
-                if k < RING - 1:
+                here = pltpu.make_async_copy(src, dst, o_recv.at[slot])
+                made.append((copy, here, chain_to == chain))
+            return made
+
+        outs = [output(h) for h in range(2)]
+
+        def put(h):
+            if h == 1:
+                for copy in detours:
+                    pl.when(crossing)(copy.start)
+            for k, (copy, here, mine) in enumerate(outs[h]):
+                if k == RING - 1:
+                    pl.when(mine)(here.start)
+                    pl.when(jnp.logical_not(mine))(copy.start)
+                elif k == RING - 2 and h == 1:
+                    pl.when(jnp.logical_not(crossing))(copy.start)
+                else:
                     copy.start()
-                    outs.append((copy, None))
-                    continue
-                here = pltpu.make_async_copy(src, dst, o_recv.at[slot])
-                mine = chain_to == chain
-                outs.append((copy, mine))
-                pl.when(mine)(here.start)
-                pl.when(jnp.logical_not(mine))(copy.start)
-
+
+        def left_out():
+            value = times((nh[...], nl[...]), factor) * (math.sqrt(2 * width) * root)
+            for s in range(2):
+                for t in range(2):
+                    obuf[0, pl.ds(2 * t + s, width, stride=4), :] = (
+                        value[s * width:(s + 1) * width, t * LANES:(t + 1) * LANES]
+                    )
+            put(0)
+
+        pl.when(jnp.logical_not(crossing))(left_out)
         carried = times(factor, split(kept[...]))
         scale_norm = norm_of(carried)
         weight_odd = jnp.log(scale_norm)
@@ -389,13 +440,13 @@
                     new_right[:, s * width + t * LANES:s * width + (t + 1) * LANES]
                 )
         put(1)
-        value = times((nh[...], nl[...]), factor) * (math.sqrt(2 * width) * root)
-        for s in range(2):
-            for t in range(2):
-                obuf[0, pl.ds(2 * t + s, width, stride=4), :] = (
-                    value[s * width:(s + 1) * width, t * LANES:(t + 1) * LANES]
-                )
-        put(0)
+        pl.when(crossing)(left_out)
+
+        @pl.when(relaying)
+        def _():
+            for c in range(2):
+                landed(held.at[pl.ds(c * short, short)], d_recv.at[c])
+                relays[c].start()
 
         for copy, dz, dk in weights:
             source = lax.rem(slab + slabs - dz, slabs) * RING + lax.rem(ring + RING - dk, RING)
@@ -421,13 +472,20 @@
         gathers_sent()
         for copy in passed + [lower]:
             copy.wait_send()
+        for copy in detours:
+            pl.when(crossing)(copy.wait_send)
+        for copy in relays:
+            pl.when(relaying)(copy.wait_send)
         for copy, dz, dk in weights:
             pl.when(slab + dz < slabs)(copy.wait_send)
-        for copy, mine in outs:
-            if mine is None:
-                copy.wait_send()
-            else:
-                pl.when(jnp.logical_not(mine))(copy.wait_send)
+        for h in range(2):
+            for k, (copy, here, mine) in enumerate(outs[h]):
+                if k == RING - 1:
+                    pl.when(jnp.logical_not(mine))(copy.wait_send)
+                elif k == RING - 2 and h == 1:
+                    pl.when(jnp.logical_not(crossing))(copy.wait_send)
+                else:
+                    copy.wait_send()
 
 
 def finish(out_ref, weights_ref, state_ref, profile_ref, held, state_sem, profile_sem):
@@ -483,6 +541,9 @@
             dma((2, RING)), dma((4,)),
             dma((slabs * RING,)), dma((slabs * RING,)),
             dma, dma,
+            pltpu.VMEM((rows * 4, LANES), jnp.float32),
+            pltpu.VMEM((2 * width // GROUPS, width), jnp.float32),
+            dma((2,)), dma((2,)), dma((2,)), dma, dma, dma,
         ],
         compiler_params=pltpu.CompilerParams(
             has_side_effects=True, collective_id=0, vmem_limit_bytes=56_000_000

time: 34.1 us -> 33.1 us (0.971); the launches traced: 33.6 us -> 33 us
  Pallas kernels: 33 us -> 32.3 us
    pallas_call x1, Pallas kernels: 32.2 us -> 31.5 us  [per_device(): pl.pallas_call(functools.partial(kernel, chains, bonds, rows, width), out...]
where the time goes in v4:
time: 33.1 us; the launch traced here: 33 us
  Pallas kernels  32.3 us (98%)
  between operations  0.64 us (2%)
    pallas_call x1, Pallas kernels, per_device(): pl.pallas_call(functools.partial(kernel, chains, bonds, rows, width), out...  31.5 us
    pallas_call x1, Pallas kernels, per_device(): pl.pallas_call(finish, out_shape=(jax.ShapeDtypeStruct(flat.shape, jnp.fl...  0.81 us

profile of v4, /device:TPU:0, one launch (start us, length us, event | category | flops | bytes accessed | tf_op | source)
XLA Modules:
  0.0 33.0 jit_solution(12414846645700820515)
XLA Ops:
  0.6 31.5 %shard_map.41 = (f32[1024,128]{1,0:T(8,128)S(1)}, f32[8,128]{1,0:T(8,128)S(1)}) custom-call(f32[1024,128]{1,0:T(8,128)} %bitcast.10, f32[4,4,4]{2,1,0:T(4,128)} %gates_ref.1), custom_call_target="tpu_custom_call" | custom-call | tf_op jit(solution)/shard_map/pallas_call | solution.py:516
  32.2 0.8 %shard_map.42 = (f32[1024,128]{1,0:T(8,128)}, f32[4]{0:T(128)}) custom-call(f32[1024,128]{1,0:T(8,128)S(1)} %get-tuple-element.6.out_ref, f32[8,128]{1,0:T(8,128)S(1)} %get-tuple-element.7.weights_ref), custom_call_target="tpu_custom_call" | custom-call | tf_op jit(solution)/shard_map/pallas_call | solution.py:552

commit v5 on v4

--- a/solution.py
+++ b/solution.py
@@ -73,14 +73,18 @@
         jnp.float32(1.5),
         jnp.float32(0.0),
     )
-    factor = None
-    for repeat in range(NS_ITERS):
-        step = eye - 0.5 * gram
-        factor = step if factor is None else times(split(factor), split(step))
-        if repeat < NS_ITERS - 1:
-            gram_split = split(gram)
-            once = 1.5 * gram - 0.5 * filled(times(gram_split, gram_split))
-            gram = 1.5 * once - 0.5 * filled(times(split(once), gram_split))
+    step = eye - 0.5 * gram
+    first, base = (split(step), split(gram))
+    square, right = (times(first, first), times(first, base))
+    filled(None)
+    right = split(right)
+    gram, cube = (times(right, first), times(split(square), right))
+    filled(None)
+    second = split(eye - 0.5 * gram)
+    both = 1.5 * step - 0.5 * cube
+    left, right = (times(split(both), second), times(second, split(gram)))
+    filled(None)
+    factor = 1.5 * both - 0.5 * filled(times(split(left), split(right)))
     while fill:
         fill.pop(0)()
     return split(factor)
@@ -234,17 +238,19 @@
             gathered(1, d)
         landed(gates.at[0], gate_recv.at[0])
         landed(gates.at[1], gate_recv.at[1])
+        pl.semaphore_wait(ring_sem, 1)
+        gathered(0, 0)
         right = jnp.concatenate([spin(1, s, 0, width) for s in range(2)], axis=1)
         bh[...], bl[...] = split(right)
         th[...], tl[...] = split(right.T)
-        pl.semaphore_wait(ring_sem, 1)
 
         gate = gates[block, 2 * (ring % 2)]
         passed = []
         squares = None
         for d in range(GROUPS):
             g = grouped(bond // part, d)
-            gathered(0, d)
+            if d:
+                gathered(0, d)
             left = jnp.concatenate([spin(0, s, g * tier, tier) for s in range(2)], axis=0)
             theta = times(split(left), (bh[...], bl[...]))
             matrix = split(mixed(theta, gate, width))
@@ -281,22 +287,25 @@
 
         gram = None
         squares = None
-        for d in range(1, GROUPS, 2):
-            parts = []
-            for e in (d - 1, d):
-                g = grouped(next_bond // part, e)
-                piece = pl.ds(g * 2 * tier, 2 * tier)
-                landed(rrecv.at[piece], m_recv.at[e])
-                parts.append(rrecv[piece, :])
-            received = jnp.concatenate(parts, axis=0)
+        pair = []
+        for d in range(GROUPS):
+            g = grouped(next_bond // part, d)
+            piece = pl.ds(g * 2 * tier, 2 * tier)
+            landed(rrecv.at[piece], m_recv.at[d])
+            received = rrecv[piece, :]
             square = sum_of_squares(received)
             squares = square if squares is None else squares + square
-            turned = split(received.T)
             piece = split(received)
-            for k, (e, s) in enumerate([(e, s) for e in (d - 1, d) for s in range(2)]):
-                g = grouped(next_bond // part, e)
-                nh[pl.ds(s * width + g * tier, tier), :] = piece[0][k * tier:(k + 1) * tier]
-                nl[pl.ds(s * width + g * tier, tier), :] = piece[1][k * tier:(k + 1) * tier]
+            for s in range(2):
+                nh[pl.ds(s * width + g * tier, tier), :] = piece[0][s * tier:(s + 1) * tier]
+                nl[pl.ds(s * width + g * tier, tier), :] = piece[1][s * tier:(s + 1) * tier]
+            pair.append((split(received.T), piece))
+            if d % 2 == 0:
+                continue
+            turned, piece = (
+                tuple(jnp.concatenate([p[k][c] for p in pair], axis=1 - k) for c in range(2)) for k in range(2)
+            )
+            pair = []
             product = times(turned, piece)
             gram = product if gram is None else gram + product
         inverse = 1.0 / (squares + EPSILON)

time: 33.1 us -> 32.8 us (level)
  no operation moved by 1% of the time
where the time goes in v5:
time: 32.8 us; the launch traced here: 32.6 us
  Pallas kernels  32 us (98%)
  between operations  0.64 us (2%)
    pallas_call x1, Pallas kernels, per_device(): pl.pallas_call(functools.partial(kernel, chains, bonds, rows, width), out...  31.2 us
    pallas_call x1, Pallas kernels, per_device(): pl.pallas_call(finish, out_shape=(jax.ShapeDtypeStruct(flat.shape, jnp.fl...  0.81 us

profile of v5, /device:TPU:0, one launch (start us, length us, event | category | flops | bytes accessed | tf_op | source)
XLA Modules:
  0.0 32.6 jit_solution(16051118247856113046)
XLA Ops:
  0.6 31.2 %shard_map.41 = (f32[1024,128]{1,0:T(8,128)S(1)}, f32[8,128]{1,0:T(8,128)S(1)}) custom-call(f32[1024,128]{1,0:T(8,128)} %bitcast.10, f32[4,4,4]{2,1,0:T(4,128)} %gates_ref.1), custom_call_target="tpu_custom_call" | custom-call | tf_op jit(solution)/shard_map/pallas_call | solution.py:525
  31.8 0.8 %shard_map.42 = (f32[1024,128]{1,0:T(8,128)}, f32[4]{0:T(128)}) custom-call(f32[1024,128]{1,0:T(8,128)S(1)} %get-tuple-element.6.out_ref, f32[8,128]{1,0:T(8,128)S(1)} %get-tuple-element.7.weights_ref), custom_call_target="tpu_custom_call" | custom-call | tf_op jit(solution)/shard_map/pallas_call | solution.py:561
